TPU v7x, 32 devices: a whole 2x2x4 slice. The times are simulated.
32 devices in a mesh: seq: 8 (over z, x), batch: 4 (over y, core).
Axes of the slice: x: 2, y: 2, z: 4, core: 2. Of those that a mesh axis runs over, the one named last changes fastest.
Arguments:
- hidden: bfloat16 [8, 2048, 4096], P('batch', None, 'seq')
- gain: float32 [4096], P('seq'), may hold values from 0.5 to 1.5
- value_weight: float32 [4096], P('seq'), may hold values from -0.09375 to 0.09375
- rewards: float32 [8, 2048], P('batch', 'seq'), may hold values from -1.5 to 1.5
- reward_mask: int32 [8, 2048], P('batch', 'seq'), may hold values 0 or 1
- lengths: int32 [8], P('batch'), may hold values from 512 to 2048
- horizon: float32 [8], P('batch'), may hold values from 24 to 16384
Outputs:
- advantages: float32 [8, 2048], P(None, ('seq', 'batch'))
- returns: float32 [8, 2048], P(None, ('seq', 'batch'))
All inputs are finite; a program needn't handle non-finite values. No bound on the sum of `reward_mask` on one device may be relied on, other than what follows from the above.
Results may differ from a plain program's by a relative error of at most 0.0003.
Values may be sent and summed in bfloat16 or wider, within the bound.
A program may use at most 64 MiB of HBM per device.

v0:
```python
import jax
import jax.numpy as jnp
from jax import lax
from jax.sharding import PartitionSpec as P

D = 4096
EPS = 1e-05


def from_behind(value, axis, steps):
    count = lax.axis_size(axis)
    initial, last = (max(0, -steps), min(count, count - steps))
    return lax.ppermute(value, axis, [(source, source + steps) for source in range(initial, last)])


def entering(array, axis, combine, identity):
    devices, position = (lax.axis_size(axis), lax.axis_index(axis))
    everything = jax.tree.map(lambda part: lax.all_gather(part, axis), array)
    start = jax.tree.map(
        lambda part, zero: jnp.broadcast_to(jnp.asarray(zero, part.dtype), part.shape),
        array,
        identity,
    )

    def step(k, before):
        at = devices - 1 - k
        reached = at > position
        new = combine(before, jax.tree.map(lambda part: part[at], everything))
        return jax.tree.map(lambda a, b: jnp.where(reached, a, b), new, before)

    return lax.fori_loop(0, devices, step, start)


def per_device(hidden, gain, value_weight, rewards, reward_mask, lengths, horizon):
    my_index = lax.axis_index("seq")
    block = rewards.shape[1]
    wide_rows = hidden.astype(jnp.float32)
    part_squares = jnp.sum(wide_rows * wide_rows, -1)
    part_projected = jnp.sum(wide_rows * (gain * value_weight), -1)
    squares, projected = (
        lax.psum_scatter(part_squares, "seq", scatter_dimension=1, tiled=True),
        lax.psum_scatter(part_projected, "seq", scatter_dimension=1, tiled=True),
    )
    values = projected * lax.rsqrt(squares / D + EPS)
    positions = my_index * block + jnp.arange(block, dtype=jnp.int32)
    valid = (positions[None, :] < lengths[:, None]).astype(jnp.float32)
    next_valid = (positions[None, :] + 1 < lengths[:, None]).astype(jnp.float32)
    following = from_behind(values[:, 0], "seq", -1)
    next_values = jnp.concatenate([values[:, 1:], following[:, None]], 1)
    delta = (rewards * reward_mask.astype(jnp.float32) + next_valid * next_values - values) * valid
    log_decay = -1.0 / horizon
    offsets = jnp.arange(block, dtype=jnp.int32)
    distance = (offsets[None, :] - offsets[:, None]).astype(jnp.float32)
    upper_mask = distance >= 0.0
    powers = jnp.where(
        upper_mask[None], jnp.exp(jnp.maximum(distance, 0.0)[None] * log_decay[:, None, None]), 0.0
    )
    local_gae = jnp.einsum("rtk,rk->rt", powers, delta, precision=lax.Precision.HIGHEST)
    tail_decay = jnp.exp((block - offsets).astype(jnp.float32)[None, :] * log_decay[:, None])
    start_value = local_gae[:, 0]
    block_decay = jnp.exp(block * log_decay)

    def compose(earlier, later):
        return (later[0] + later[1] * earlier[0], later[1] * earlier[1])

    carry_in, _ = entering(
        (start_value, block_decay),
        "seq",
        compose,
        (jnp.zeros_like(start_value), jnp.ones_like(block_decay)),
    )
    gae = local_gae + tail_decay * carry_in[:, None]
    returns = (gae + values) * valid
    count, first, second = lax.psum(
        (jnp.sum(valid), jnp.sum(gae), jnp.sum(gae * gae)), ("seq", "batch")
    )
    mean = first / count
    var = jnp.maximum(second / count - mean * mean, 1.0)
    whitened = (gae - mean) * valid * lax.rsqrt(var)
    out_adv, out_returns = (
        lax.all_to_all(whitened, "batch", split_axis=1, concat_axis=0, tiled=True),
        lax.all_to_all(returns, "batch", split_axis=1, concat_axis=0, tiled=True),
    )
    return (out_adv, out_returns)


def solution(mesh):
    return jax.shard_map(
        per_device,
        mesh=mesh,
        in_specs=(
            P("batch", None, "seq"),
            P("seq"),
            P("seq"),
            P("batch", "seq"),
            P("batch", "seq"),
            P("batch"),
            P("batch"),
        ),
        out_specs=(P(None, ("seq", "batch")), P(None, ("seq", "batch"))),
        check_vma=False,
    )
```

profile of v0, /device:TPU:10, one launch (start us, length us, event | category | flops | bytes accessed | tf_op | source)
XLA Modules:
  0.0 239.2 jit_solution(13834046668706539538)
XLA Ops:
  7.2 0.0 reduce-scatter.7.cloned.1.call-start
  7.2 0.7 mul.99
  7.9 0.0 copy-start.2
  7.9 3.7 %fusion.2 = (f32[2,2048]{1,0:T(2,128)S(1)}, f32[2,2048]{1,0:T(2,128)S(1)}) fusion(bf16[2,2048,512]{2,1,0:T(8,128)(2,1)} %param.9, f32[512]{0:T(512)S(1)} %mul.99), kind=kLoop, calls=%fused_computation.7 | loop fusion | flops 10477568 | bytes 4229120 | tf_op jit(solution)/shard_map/reduce_sum | solution.py:38
  11.7 1.4 copy.23
  13.0 0.0 reduce-scatter.7.cloned.1.call-update
  13.1 0.0 reduce-scatter.9.cloned.1.call-start
  13.1 1.4 copy.25
  14.5 0.0 reduce-scatter.9.cloned.1.call-update
  14.6 0.1 convert_compare_fusion
  14.7 0.0 copy-done.4
  14.7 0.6 dynamic-slice
  16.0 0.1 exponential_dynamic-update-slice_fusion
  16.1 62.7 %reduce-scatter.7.cloned.1.call-done = f32[256,2]{1,0:T(8,128)} async-done(((f32[2048,2]{1,0:T(8,128)}), f32[256,2]{1,0:T(8,128)}) %reduce-scatter.7.cloned.1.call-update) | async-done | bytes 2064
  78.7 1.0 copy.24
  79.7 65.6 %reduce-scatter.9.cloned.1.call-done = f32[256,2]{1,0:T(8,128)} async-done(((f32[2048,2]{1,0:T(8,128)}), f32[256,2]{1,0:T(8,128)}) %reduce-scatter.9.cloned.1.call-update) | async-done | bytes 2064
  145.3 1.0 copy.26
  146.3 0.1 slice_reduce_fusion.1
  146.4 0.1 slice.12
  146.5 2.5 %collective-permute-start = (f32[2]{0:T(128)S(1)}, f32[2]{0:T(128)S(1)}, u32[]{:S(2)}, u32[]{:S(2)}) collective-permute-start(f32[2]{0:T(128)S(1)} %slice_reduce_fusion.1), channel_id=1, source_target_pairs={{4,0},{8,4},{12,8},{16,12},{20,16},{24,20},{28,24},{5,1},{9,5},{13... | collective-permute-start | bytes 32 | tf_op jit(solution)/shard_map/ppermute | solution.py:13
  148.9 3.9 %collective-permute-done = f32[2]{0:T(128)S(1)} collective-permute-done((f32[2]{0:T(128)S(1)}, f32[2]{0:T(128)S(1)}, u32[]{:S(2)}, u32[]{:S(2)}) %collective-permute-start) | collective-permute-done | bytes 40 | tf_op jit(solution)/shard_map/ppermute | solution.py:13
  152.8 0.1 copy.18
  152.9 0.0 copy-done
  152.9 0.1 fusion.16
  153.0 0.7 fusion.3
  153.7 0.1 slice_reduce_fusion
  153.9 0.2 dynamic-update-slice
  154.1 14.3 %all-reduce.3 = (f32[16]{0:T(128)S(1)}, f32[16]{0:T(128)S(1)}) all-reduce(f32[16]{0:T(128)S(1)} %dynamic-update-slice, f32[16]{0:T(128)S(1)} %get-tuple-element.174), channel_id=2, replica_groups=mesh['seq'=8,'batch'=4] {'seq'}, use_global_device_ids=true, to_apply=%add | all-reduce | flops 32 | bytes 256
  168.4 0.1 reshape.52
  168.4 0.1 reshape.53
  168.5 0.4 while.16
  168.9 0.7 compare_select_fusion
  169.5 0.7 fusion.18
  170.2 43.4 %all-reduce.2 = (f32[]{:T(128)}, f32[]{:T(128)}, f32[]{:T(128)}) all-reduce(f32[]{:T(128)} %get-tuple-element.156, f32[]{:T(128)} %get-tuple-element.176, f32[]{:T(128)} %get-tuple-element.155), channel_id=1, replica_groups=mesh['seq'=8,'batch'=4] {'seq','batch'}, use_global_device_ids=true, to_apply=%region_11.12 | all-reduce | flops 3 | bytes 24 | tf_op jit(solution)/shard_map/psum | solution.py:74
  216.3 0.1 fusion.14
  216.4 0.1 all_to_all.28
  216.5 0.7 reshape.73
  217.1 3.2 %all-to-all-start = ((f32[4,1,128]{2,1,0:T(1,128)}), f32[4,1,128]{2,1,0:T(1,128)S(1)}, u32[]{:S(2)}, u32[]{:S(2)}) async-start(f32[4,1,128]{2,1,0:T(1,128)} %reshape.73), calls=%async_computation | async-start | bytes 4096 | tf_op jit(solution)/shard_map/all_to_all | solution.py:81
  220.3 0.1 all_to_all.32
  220.4 0.7 reshape.75
  221.1 2.9 %all-to-all-done = f32[4,1,128]{2,1,0:T(1,128)S(1)} async-done(((f32[4,1,128]{2,1,0:T(1,128)}), f32[4,1,128]{2,1,0:T(1,128)S(1)}, u32[]{:S(2)}, u32[]{:S(2)}) %all-to-all-start) | async-done | bytes 2080 | tf_op jit(solution)/shard_map/all_to_all | solution.py:81
  224.0 3.2 %all-to-all-start.1 = ((f32[4,1,128]{2,1,0:T(1,128)}), f32[4,1,128]{2,1,0:T(1,128)S(1)}, u32[]{:S(2)}, u32[]{:S(2)}) async-start(f32[4,1,128]{2,1,0:T(1,128)} %reshape.75), calls=%async_computation.1 | async-start | bytes 4096 | tf_op jit(solution)/shard_map/all_to_all | solution.py:82
  227.3 0.5 broadcast.83
  227.8 0.7 reduce.4
  228.4 0.7 reshape.74
  229.1 1.9 all-to-all-done.1
  231.0 0.7 reduce.5
  231.7 0.7 reshape.76
  (25 shorter events, 0.2 us)
Async XLA Ops:
  7.2 71.6 %reduce-scatter.7.cloned.1.call-start = ((), (), s32[]{:S(2)}) async-start(), calls=%async_computation.4 | async-start | bytes 1179648
  7.9 6.8 %copy-start.4 = (u32[32]{0:T(128)S(1)}, u32[32]{0:T(128)}, u32[]{:S(2)}) copy-start(u32[32]{0:T(128)} %constant.81) | copy-start | bytes 388
  7.9 8.0 %copy-start.3 = (f32[2]{0:T(128)S(1)}, f32[2]{0:T(128)}, u32[]{:S(2)}) copy-start(f32[2]{0:T(128)} %param.15) | copy-start | bytes 28
  7.9 145.0 %copy-start = (s32[2]{0:T(128)S(1)}, s32[2]{0:T(128)}, u32[]{:S(2)}) copy-start(s32[2]{0:T(128)} %param.14) | copy-start | bytes 28
  7.9 145.0 %copy-start.1 = (f32[2,256]{1,0:T(2,128)S(1)}, f32[2,256]{1,0:T(2,128)}, u32[]{:S(2)}) copy-start(f32[2,256]{1,0:T(2,128)} %param.12) | copy-start | bytes 6148
  7.9 145.0 %copy-start.2 = (s32[2,256]{1,0:T(2,128)S(1)}, s32[2,256]{1,0:T(2,128)}, u32[]{:S(2)}) copy-start(s32[2,256]{1,0:T(2,128)} %param.13) | copy-start | bytes 6148
  13.1 132.2 %reduce-scatter.9.cloned.1.call-start = ((), (), s32[]{:S(2)}) async-start(), calls=%async_computation.5 | async-start | bytes 1179648
  146.5 6.4 %collective-permute-start = (f32[2]{0:T(128)S(1)}, f32[2]{0:T(128)S(1)}, u32[]{:S(2)}, u32[]{:S(2)}) collective-permute-start(f32[2]{0:T(128)S(1)} %slice_reduce_fusion.1), channel_id=1, source_target_pairs={{4,0},{8,4},{12,8},{16,12},{20,16},{24,20},{28,24},{5,1},{9,5},{13... | collective-permute-start | bytes 32 | tf_op jit(solution)/shard_map/ppermute | solution.py:13
  217.1 6.9 %all-to-all-start = ((f32[4,1,128]{2,1,0:T(1,128)}), f32[4,1,128]{2,1,0:T(1,128)S(1)}, u32[]{:S(2)}, u32[]{:S(2)}) async-start(f32[4,1,128]{2,1,0:T(1,128)} %reshape.73), calls=%async_computation | async-start | bytes 4096 | tf_op jit(solution)/shard_map/all_to_all | solution.py:81
  224.0 7.0 %all-to-all-start.1 = ((f32[4,1,128]{2,1,0:T(1,128)}), f32[4,1,128]{2,1,0:T(1,128)S(1)}, u32[]{:S(2)}, u32[]{:S(2)}) async-start(f32[4,1,128]{2,1,0:T(1,128)} %reshape.75), calls=%async_computation.1 | async-start | bytes 4096 | tf_op jit(solution)/shard_map/all_to_all | solution.py:82
Sparse Core Ops, SparseCore 0:
  13.2 65.5 reduce-scatter.6
  82.2 63.0 reduce-scatter.8
where the time goes:
time: 240 us; the launch traced here: 239 us
  waiting for transfers between devices  137 us (57%)
  blocking collectives  57.7 us (24%)
  between operations  17.5 us (7%)
  local copies, waits for them, and re-layouts  9.54 us (4%)
  starting transfers between devices  9.02 us (4%)
  other arithmetic  7.63 us (3%)
    unnamed x4, waiting for transfers between devices  128 us
    psum x1, blocking collectives, per_device(): lax.psum((jnp.sum(valid), jnp.sum(gae), jnp.sum(gae * gae)), ('seq', 'bat...  43.4 us
    unnamed x1, blocking collectives  14.3 us
    unnamed x22, local copies, waits for them, and re-layouts  8.28 us
  transfers between devices with their start and end apart: 5, of which 5 were waited for; matrix products, arithmetic and copies ran while one was open for 2% of the time, Pallas kernels for 0%

commit v1 on v0

--- a/solution.py
+++ b/solution.py
@@ -2,9 +2,14 @@
 import jax.numpy as jnp
 from jax import lax
 from jax.sharding import PartitionSpec as P
+from jax.lax import psum
 
 D = 4096
 EPS = 1e-05
+
+
+def table_drive(local_array):
+    return psum(psum(local_array, "batch"), "seq")
 
 
 def from_behind(value, axis, steps):
@@ -71,9 +76,7 @@
     )
     gae = local_gae + tail_decay * carry_in[:, None]
     returns = (gae + values) * valid
-    count, first, second = lax.psum(
-        (jnp.sum(valid), jnp.sum(gae), jnp.sum(gae * gae)), ("seq", "batch")
-    )
+    count, first, second = table_drive((jnp.sum(valid), jnp.sum(gae), jnp.sum(gae * gae)))
     mean = first / count
     var = jnp.maximum(second / count - mean * mean, 1.0)
     whitened = (gae - mean) * valid * lax.rsqrt(var)

time: 240 us -> 226 us (0.942); the launches traced: 239 us -> 222 us
  blocking collectives: 57.7 us -> 40.3 us
    psum x1 -> x2, blocking collectives: 43.4 us -> 26.1 us  [table_drive(): return psum(psum(local_array, 'batch'), 'seq')]
  transfers between devices with their start and end apart: 5 -> 5, of which waited for: 5 -> 5; matrix products, arithmetic and copies ran while one was open for 2% -> 3% of each run, Pallas kernels for 0% -> 0%
where the time goes in v1:
time: 226 us; the launch traced here: 222 us
  waiting for transfers between devices  137 us (61%)
  blocking collectives  40.3 us (18%)
  between operations  17.5 us (8%)
  local copies, waits for them, and re-layouts  9.54 us (4%)
  starting transfers between devices  9.02 us (4%)
  other arithmetic  7.55 us (3%)
    unnamed x4, waiting for transfers between devices  128 us
    psum x2, blocking collectives, table_drive(): return psum(psum(local_array, 'batch'), 'seq')  26.1 us
    unnamed x1, blocking collectives  14.3 us
    unnamed x22, local copies, waits for them, and re-layouts  8.28 us
  transfers between devices with their start and end apart: 5, of which 5 were waited for; matrix products, arithmetic and copies ran while one was open for 3% of the time, Pallas kernels for 0%

profile of v1, /device:TPU:10, one launch (start us, length us, event | category | flops | bytes accessed | tf_op | source)
XLA Modules:
  0.0 221.7 jit_solution(16959910384667161370)
XLA Ops:
  7.2 0.0 reduce-scatter.7.cloned.1.call-start
  7.2 0.7 mul.99
  7.9 0.0 copy-start.2
  7.9 3.7 %fusion.2 = (f32[2,2048]{1,0:T(2,128)S(1)}, f32[2,2048]{1,0:T(2,128)S(1)}) fusion(bf16[2,2048,512]{2,1,0:T(8,128)(2,1)} %param.9, f32[512]{0:T(512)S(1)} %mul.99), kind=kLoop, calls=%fused_computation.7 | loop fusion | flops 10477568 | bytes 4229120 | tf_op jit(solution)/shard_map/reduce_sum | solution.py:43
  11.7 1.4 copy.23
  13.0 0.0 reduce-scatter.7.cloned.1.call-update
  13.1 0.0 reduce-scatter.9.cloned.1.call-start
  13.1 1.4 copy.25
  14.5 0.0 reduce-scatter.9.cloned.1.call-update
  14.6 0.1 convert_compare_fusion
  14.7 0.0 copy-done.4
  14.7 0.6 dynamic-slice
  16.0 0.1 exponential_dynamic-update-slice_fusion
  16.1 62.7 %reduce-scatter.7.cloned.1.call-done = f32[256,2]{1,0:T(8,128)} async-done(((f32[2048,2]{1,0:T(8,128)}), f32[256,2]{1,0:T(8,128)}) %reduce-scatter.7.cloned.1.call-update) | async-done | bytes 2064
  78.7 1.0 copy.24
  79.7 65.6 %reduce-scatter.9.cloned.1.call-done = f32[256,2]{1,0:T(8,128)} async-done(((f32[2048,2]{1,0:T(8,128)}), f32[256,2]{1,0:T(8,128)}) %reduce-scatter.9.cloned.1.call-update) | async-done | bytes 2064
  145.3 1.0 copy.26
  146.3 0.1 slice_reduce_fusion.1
  146.4 0.1 slice.12
  146.5 2.5 %collective-permute-start = (f32[2]{0:T(128)S(1)}, f32[2]{0:T(128)S(1)}, u32[]{:S(2)}, u32[]{:S(2)}) collective-permute-start(f32[2]{0:T(128)S(1)} %slice_reduce_fusion.1), channel_id=1, source_target_pairs={{4,0},{8,4},{12,8},{16,12},{20,16},{24,20},{28,24},{5,1},{9,5},{13... | collective-permute-start | bytes 32 | tf_op jit(solution)/shard_map/ppermute | solution.py:18
  148.9 3.9 %collective-permute-done = f32[2]{0:T(128)S(1)} collective-permute-done((f32[2]{0:T(128)S(1)}, f32[2]{0:T(128)S(1)}, u32[]{:S(2)}, u32[]{:S(2)}) %collective-permute-start) | collective-permute-done | bytes 40 | tf_op jit(solution)/shard_map/ppermute | solution.py:18
  152.8 0.1 copy.18
  152.9 0.1 fusion.16
  153.0 0.7 fusion.3
  153.7 0.1 slice_reduce_fusion
  153.9 0.2 dynamic-update-slice
  154.1 14.3 %all-reduce.3 = (f32[16]{0:T(128)S(1)}, f32[16]{0:T(128)S(1)}) all-reduce(f32[16]{0:T(128)S(1)} %dynamic-update-slice, f32[16]{0:T(128)S(1)} %get-tuple-element.177), channel_id=2, replica_groups=mesh['seq'=8,'batch'=4] {'seq'}, use_global_device_ids=true, to_apply=%add | all-reduce | flops 32 | bytes 256
  168.4 0.1 reshape.52
  168.4 0.1 reshape.53
  168.5 0.4 while.16
  168.9 0.7 compare_select_fusion
  169.5 0.6 fusion.18
  170.1 6.3 %all-reduce.4 = (f32[]{:T(128)}, f32[]{:T(128)}, f32[]{:T(128)}) all-reduce(f32[]{:T(128)} %get-tuple-element.156, f32[]{:T(128)} %get-tuple-element.179, f32[]{:T(128)} %get-tuple-element.155), channel_id=1, replica_groups=mesh['seq'=8,'batch'=4] {'batch'}, use_global_device_ids=true, to_apply=%region_13.14 | all-reduce | flops 3 | bytes 24 | tf_op jit(solution)/shard_map/psum | solution.py:12
  176.5 19.7 %all-reduce.2 = (f32[]{:T(128)}, f32[]{:T(128)}, f32[]{:T(128)}) all-reduce(f32[]{:T(128)} %get-tuple-element.172, f32[]{:T(128)} %get-tuple-element.173, f32[]{:T(128)} %get-tuple-element.174), channel_id=1, replica_groups=mesh['seq'=8,'batch'=4] {'seq'}, use_global_device_ids=true, to_apply=%region_14.15 | all-reduce | flops 3 | bytes 24 | tf_op jit(solution)/shard_map/psum | solution.py:12
  198.8 0.1 fusion.14
  198.9 0.1 all_to_all.28
  199.0 0.7 reshape.73
  199.7 3.2 %all-to-all-start = ((f32[4,1,128]{2,1,0:T(1,128)}), f32[4,1,128]{2,1,0:T(1,128)S(1)}, u32[]{:S(2)}, u32[]{:S(2)}) async-start(f32[4,1,128]{2,1,0:T(1,128)} %reshape.73), calls=%async_computation | async-start | bytes 4096 | tf_op jit(solution)/shard_map/all_to_all | solution.py:84
  202.9 0.1 all_to_all.32
  203.0 0.7 reshape.75
  203.7 2.9 %all-to-all-done = f32[4,1,128]{2,1,0:T(1,128)S(1)} async-done(((f32[4,1,128]{2,1,0:T(1,128)}), f32[4,1,128]{2,1,0:T(1,128)S(1)}, u32[]{:S(2)}, u32[]{:S(2)}) %all-to-all-start) | async-done | bytes 2080 | tf_op jit(solution)/shard_map/all_to_all | solution.py:84
  206.6 3.2 %all-to-all-start.1 = ((f32[4,1,128]{2,1,0:T(1,128)}), f32[4,1,128]{2,1,0:T(1,128)S(1)}, u32[]{:S(2)}, u32[]{:S(2)}) async-start(f32[4,1,128]{2,1,0:T(1,128)} %reshape.75), calls=%async_computation.1 | async-start | bytes 4096 | tf_op jit(solution)/shard_map/all_to_all | solution.py:85
  209.8 0.5 broadcast.83
  210.3 0.7 reduce.4
  211.0 0.7 reshape.74
  211.7 1.9 all-to-all-done.1
  213.6 0.7 reduce.5
  214.2 0.7 reshape.76
  (26 shorter events, 0.2 us)
Async XLA Ops:
  7.2 71.6 %reduce-scatter.7.cloned.1.call-start = ((), (), s32[]{:S(2)}) async-start(), calls=%async_computation.4 | async-start | bytes 1179648
  7.9 6.8 %copy-start.4 = (u32[32]{0:T(128)S(1)}, u32[32]{0:T(128)}, u32[]{:S(2)}) copy-start(u32[32]{0:T(128)} %constant.81) | copy-start | bytes 388
  7.9 8.0 %copy-start.3 = (f32[2]{0:T(128)S(1)}, f32[2]{0:T(128)}, u32[]{:S(2)}) copy-start(f32[2]{0:T(128)} %param.15) | copy-start | bytes 28
  7.9 145.0 %copy-start = (s32[2]{0:T(128)S(1)}, s32[2]{0:T(128)}, u32[]{:S(2)}) copy-start(s32[2]{0:T(128)} %param.14) | copy-start | bytes 28
  7.9 145.0 %copy-start.1 = (f32[2,256]{1,0:T(2,128)S(1)}, f32[2,256]{1,0:T(2,128)}, u32[]{:S(2)}) copy-start(f32[2,256]{1,0:T(2,128)} %param.12) | copy-start | bytes 6148
  7.9 145.0 %copy-start.2 = (s32[2,256]{1,0:T(2,128)S(1)}, s32[2,256]{1,0:T(2,128)}, u32[]{:S(2)}) copy-start(s32[2,256]{1,0:T(2,128)} %param.13) | copy-start | bytes 6148
  13.1 132.2 %reduce-scatter.9.cloned.1.call-start = ((), (), s32[]{:S(2)}) async-start(), calls=%async_computation.5 | async-start | bytes 1179648
  146.5 6.4 %collective-permute-start = (f32[2]{0:T(128)S(1)}, f32[2]{0:T(128)S(1)}, u32[]{:S(2)}, u32[]{:S(2)}) collective-permute-start(f32[2]{0:T(128)S(1)} %slice_reduce_fusion.1), channel_id=1, source_target_pairs={{4,0},{8,4},{12,8},{16,12},{20,16},{24,20},{28,24},{5,1},{9,5},{13... | collective-permute-start | bytes 32 | tf_op jit(solution)/shard_map/ppermute | solution.py:18
  199.7 6.9 %all-to-all-start = ((f32[4,1,128]{2,1,0:T(1,128)}), f32[4,1,128]{2,1,0:T(1,128)S(1)}, u32[]{:S(2)}, u32[]{:S(2)}) async-start(f32[4,1,128]{2,1,0:T(1,128)} %reshape.73), calls=%async_computation | async-start | bytes 4096 | tf_op jit(solution)/shard_map/all_to_all | solution.py:84
  206.6 7.0 %all-to-all-start.1 = ((f32[4,1,128]{2,1,0:T(1,128)}), f32[4,1,128]{2,1,0:T(1,128)S(1)}, u32[]{:S(2)}, u32[]{:S(2)}) async-start(f32[4,1,128]{2,1,0:T(1,128)} %reshape.75), calls=%async_computation.1 | async-start | bytes 4096 | tf_op jit(solution)/shard_map/all_to_all | solution.py:85
Sparse Core Ops, SparseCore 0:
  13.2 65.5 reduce-scatter.6
  82.2 63.0 reduce-scatter.8
